TPU v7x, 32 devices: a whole 2x2x4 slice. The times are simulated.
32 devices in a mesh: head: 8 (over z, core), kv: 4 (over y, x).
Axes of the slice: x: 2, y: 2, z: 4, core: 2. Of those that a mesh axis runs over, the one named last changes fastest.
Arguments:
- queries: bfloat16 [2048, 8192], P(('kv', 'head')), may hold values from -6 to 6
- key_rows: bfloat16 [2048, 1024], P(('kv', 'head')), may hold values from -6 to 6
- value_matrix: bfloat16 [2048, 1024], P(('kv', 'head')), may hold values from -6 to 6
- doc_ids: int32 [2048], P(('kv', 'head')), may hold values from 0 to 5, as said below
Outputs:
- attended: bfloat16 [2048, 8192], P(('kv', 'head'))
Inputs may be any that keep to these rules, and one draw needn't show every extreme that they name: doc_ids starts at 0, never falls, and rises by one at the first token of each of the 6 documents; every document starts at an even position and has 2 tokens or more.
All inputs are finite; a program needn't handle non-finite values.
Results may differ from a plain program's by a relative error of at most 0.015.
Values may be sent and summed in bfloat16 or wider, within the bound.
A program may use at most 64 MiB of HBM per device.

v0:
```python
import math
import jax
import jax.numpy as jnp
from jax import lax
from jax.sharding import PartitionSpec as P

QUERY_HEADS = 64
KEY_VALUE_HEADS = 8
HEAD_SIZE = 128
NEG_FILL = -1e30


def repeat_heads(input_matrix, head_repeats):
    row_number = input_matrix.shape[0]
    heads_apart = input_matrix.reshape(row_number, KEY_VALUE_HEADS, 1, HEAD_SIZE)
    expanded_heads = jnp.broadcast_to(
        heads_apart, (row_number, KEY_VALUE_HEADS, head_repeats, HEAD_SIZE)
    )
    return expanded_heads.reshape(row_number, KEY_VALUE_HEADS * head_repeats * HEAD_SIZE)


def block_terms(query_group, query_pos, query_doc, key_block, value_block, key_pos, key_doc):
    key_count = key_block.shape[0]
    key_value_slot = query_group.shape[1]
    key_heads = key_block.reshape(key_count, key_value_slot, HEAD_SIZE)
    value_heads = value_block.reshape(key_count, key_value_slot, HEAD_SIZE)
    scores = jnp.einsum(
        "rkgd,ckd->kgrc", query_group, key_heads, preferred_element_type=jnp.float32
    ) * HEAD_SIZE ** (-0.5)
    allowed = (key_pos[None, :] <= query_pos[:, None]) & (key_doc[None, :] == query_doc[:, None])
    masked = jnp.where(allowed, scores, NEG_FILL)
    row_peak = jnp.max(masked, axis=-1)
    weights = jnp.where(allowed, jnp.exp(masked - row_peak[..., None]), 0.0)
    row_total = jnp.sum(weights, axis=-1)
    weighted = jnp.einsum(
        "kgrc,ckd->kgrd",
        weights.astype(jnp.bfloat16),
        value_heads,
        preferred_element_type=jnp.float32,
    )
    return (row_peak, row_total, weighted)


def attend_block(query_group, query_pos, query_doc, key_block, value_block, key_pos, key_doc):
    return block_terms(query_group, query_pos, query_doc, key_block, value_block, key_pos, key_doc)


def combine_terms(first_terms, second_terms):
    joint_peak = jnp.maximum(first_terms[0], second_terms[0])
    left_factor = jnp.exp(first_terms[0] - joint_peak)
    right_factor = jnp.exp(second_terms[0] - joint_peak)
    joint_total = first_terms[1] * left_factor + second_terms[1] * right_factor
    joint_weighted = (
        first_terms[2] * left_factor[..., None] + second_terms[2] * right_factor[..., None]
    )
    return (joint_peak, joint_total, joint_weighted)


def local(queries, key_rows, value_matrix, doc_ids):
    head_number = lax.axis_size("head")
    head_repeats = max(1, head_number // KEY_VALUE_HEADS)
    key_send = repeat_heads(key_rows, head_repeats)
    value_send = repeat_heads(value_matrix, head_repeats)
    query_block, key_block, value_block = (
        lax.all_to_all(queries, "head", split_axis=1, concat_axis=0, tiled=True),
        lax.all_to_all(key_send, "head", split_axis=1, concat_axis=0, tiled=True),
        lax.all_to_all(value_send, "head", split_axis=1, concat_axis=0, tiled=True),
    )
    block_len = query_block.shape[0]
    doc_global = lax.all_gather(doc_ids, ("kv", "head"), axis=0, tiled=True)
    query_width = query_block.shape[1]
    present_heads = query_width // HEAD_SIZE
    key_value_slot = max(1, present_heads // (QUERY_HEADS // KEY_VALUE_HEADS))
    group_here = present_heads // key_value_slot
    own_first = lax.axis_index("kv") * block_len
    own_pos = own_first + jnp.arange(block_len, dtype=jnp.int32)
    own_doc = jnp.take(doc_global, own_pos)
    query_group = query_block.reshape(block_len, key_value_slot, group_here, HEAD_SIZE)
    term_shape = (key_value_slot, group_here, block_len)
    initial = (
        jnp.full(term_shape, NEG_FILL, jnp.float32),
        jnp.zeros(term_shape, jnp.float32),
        jnp.zeros(term_shape + (HEAD_SIZE,), jnp.float32),
    )
    key_piece = lax.all_gather(key_block, "kv", axis=0, tiled=True)
    value_piece = lax.all_gather(value_block, "kv", axis=0, tiled=True)
    piece_rows = key_piece.shape[0]
    step_rows = math.gcd(piece_rows, 1024)

    def one_step(step_index, inner):
        local_first = step_index * step_rows
        keys_now = lax.dynamic_slice_in_dim(key_piece, local_first, step_rows, 0)
        values_now = lax.dynamic_slice_in_dim(value_piece, local_first, step_rows, 0)
        key_pos = local_first + jnp.arange(step_rows, dtype=jnp.int32)
        key_doc = jnp.take(doc_global, key_pos)
        return combine_terms(
            inner,
            attend_block(query_group, own_pos, own_doc, keys_now, values_now, key_pos, key_doc),
        )

    folded = lax.fori_loop(0, piece_rows // step_rows, one_step, initial)
    result = (
        (folded[2] / folded[1][..., None]).transpose(2, 0, 1, 3).reshape(block_len, query_width)
    )
    result = result.astype(jnp.bfloat16)
    return lax.all_to_all(result, "head", split_axis=0, concat_axis=1, tiled=True)


def solution(mesh):
    return jax.shard_map(
        local,
        mesh=mesh,
        in_specs=(
            P(("kv", "head"), None),
            P(("kv", "head"), None),
            P(("kv", "head"), None),
            P(("kv", "head")),
        ),
        out_specs=P(("kv", "head"), None),
        check_vma=False,
    )
```

profile of v0, /device:TPU:0, one launch (start us, length us, event | category | flops | bytes accessed | tf_op | source)
XLA Modules:
  0.0 176.7 jit_solution(10033229204570758715)
XLA Ops:
  0.0 0.0 copy-start
  0.0 0.9 copy-done
  0.9 0.7 copy_bitcast_fusion.2
  1.6 6.4 %all-to-all-start = ((bf16[64,8,128]{2,0,1:T(8,128)(2,1)}), bf16[64,8,128]{2,0,1:T(8,128)(2,1)S(1)}, u32[]{:S(2)}, u32[]{:S(2)}) async-start(bf16[64,8,128]{2,0,1:T(8,128)(2,1)} %copy_bitcast_fusion.2), calls=%async_computation | async-start | bytes 262144 | tf_op jit(solution)/shard_map/all_to_all | solution.py:66
  7.9 1.6 copy_bitcast_fusion.1
  9.5 5.2 %all-to-all-done = bf16[64,8,128]{2,0,1:T(8,128)(2,1)S(1)} async-done(((bf16[64,8,128]{2,0,1:T(8,128)(2,1)}), bf16[64,8,128]{2,0,1:T(8,128)(2,1)S(1)}, u32[]{:S(2)}, u32[]{:S(2)}) %all-to-all-start) | async-done | bytes 131104 | tf_op jit(solution)/shard_map/all_to_all | solution.py:66
  14.7 3.4 %all-to-all-start.2 = ((bf16[64,8,128]{2,0,1:T(8,128)(2,1)}), bf16[64,8,128]{2,0,1:T(8,128)(2,1)S(1)}, u32[]{:S(2)}, u32[]{:S(2)}) async-start(bf16[64,8,128]{2,0,1:T(8,128)(2,1)} %copy_bitcast_fusion.1), calls=%async_computation.2 | async-start | bytes 262144 | tf_op jit(solution)/shard_map/all_to_all | solution.py:67
  18.1 2.3 %copy.30 = bf16[8,8,8,1024]{3,2,0,1:T(8,128)(2,1)} copy(bf16[8,8,8,1024]{3,2,1,0:T(8,128)(2,1)} %bitcast.121) | data formatting | bytes 2097152 | tf_op jit(solution)/shard_map/all_to_all | solution.py:65
  20.4 4.4 %all-to-all-done.2 = bf16[64,8,128]{2,0,1:T(8,128)(2,1)S(1)} async-done(((bf16[64,8,128]{2,0,1:T(8,128)(2,1)}), bf16[64,8,128]{2,0,1:T(8,128)(2,1)S(1)}, u32[]{:S(2)}, u32[]{:S(2)}) %all-to-all-start.2) | async-done | bytes 131104 | tf_op jit(solution)/shard_map/all_to_all | solution.py:67
  24.8 3.6 %all-to-all-start.1 = ((bf16[64,8,1024]{2,0,1:T(8,128)(2,1)}), bf16[64,8,1024]{2,0,1:T(8,128)(2,1)S(1)}, u32[]{:S(2)}, u32[]{:S(2)}) async-start(bf16[64,8,1024]{2,0,1:T(8,128)(2,1)} %bitcast.93), calls=%async_computation.1 | async-start | bytes 2097152 | tf_op jit(solution)/shard_map/all_to_all | solution.py:65
  28.4 1.3 dynamic-slice
  30.4 0.9 dynamic-update-slice
  31.2 43.9 %all-reduce = s32[2048]{0:T(1024)S(1)} all-reduce(s32[2048]{0:T(1024)S(1)} %dynamic-update-slice), channel_id=1, replica_groups=mesh['head'=8,'kv'=4] {'kv','head'}, use_global_device_ids=true, to_apply=%add | all-reduce | flops 2048 | bytes 16384
  75.2 3.1 %gather_fusion.1 = s32[512]{0:T(512)S(1)} fusion(s32[2048]{0:T(1024)S(1)} %all-reduce, s32[1024]{0:T(1024)S(1)} %pad_clamp_fusion), kind=kCustom, calls=%fused_computation.1 | custom fusion | bytes 6144 | tf_op jit(solution)/shard_map/jit(_take)/gather | solution.py:77
  78.3 11.6 %all_gather.11 = bf16[2048,128]{1,0:T(8,128)(2,1)S(1)} all-gather(bf16[512,128]{1,0:T(8,128)(2,1)S(1)} %bitcast.124), channel_id=1, replica_groups=mesh['head'=8,'kv'=4] {'kv'}, dimensions={0}, use_global_device_ids=true | all-gather | bytes 655360 | tf_op jit(solution)/shard_map/all_gather | solution.py:86
  89.9 9.0 %all_gather.10 = bf16[2048,128]{1,0:T(8,128)(2,1)S(1)} all-gather(bf16[512,128]{1,0:T(8,128)(2,1)S(1)} %bitcast.123), channel_id=1, replica_groups=mesh['head'=8,'kv'=4] {'kv'}, dimensions={0}, use_global_device_ids=true | all-gather | bytes 655360 | tf_op jit(solution)/shard_map/all_gather | solution.py:85
  98.9 0.0 all-to-all-done.1
  98.9 0.3 copy.26
  99.2 0.1 copy.18
  99.3 43.2 %while.18 = (s32[]{:T(128)}, f32[1,8,512]{2,1,0:T(8,128)S(1)}, f32[1,8,512]{2,1,0:T(8,128)S(1)}, f32[1,8,512,128]{3,2,1,0:T(8,128)}, s32[2048]{0:T(1024)S(1)}, /...) while((s32[]{:T(128)}, f32[1,8,512]{2,1,0:T(8,128)S(1)}, ...), condition=%wide.region_3.4_spmd.clone, body=%wide.region_0.3_spmd.clone.sunk | while | flops 2205726208 | bytes 75335952 | solution.py:101
  99.4 6.2 %gather_fusion = s32[1024]{0:T(1024)S(1)} fusion(s32[2048]{0:T(1024)S(1)} %get-tuple-element.370, s32[1024]{0:T(1024)S(1)} %broadcast_clamp_fusion.2), kind=kCustom, calls=%fused_computation.clone.clone.1 | custom fusion | bytes 12288 | tf_op jit(solution)/shard_map/while/body/eval_jaxpr/jit(_take)/gather | solution.py:95
  105.6 0.8 compare_and_fusion.2
  106.4 2.9 %fusion.41 = (f32[8,512]{1,0:T(8,128)S(1)}, f32[1024,512,8]{1,0,2:T(8,128)S(1)}) fusion(pred[512,1024]{0,1:T(8,128)(4,1)S(1)} %compare_and_fusion.2, bf16[512,1,8,128]{3,0,2,1:T(8,128)(2,1)S(1)} %get-tuple-element.373, bf16[2048,128]{1,0:T(8,128)(2,1)S(1)} %get-tuple-element.372, s32[]{:T(128)S(6)} %select_n.145), kind=kOutput, calls=%fused_computation.5.clone.1 | convolution fusion | flops 1086320640 | bytes 18628612 | tf_op jit(solution)/shard_map/while/body/eval_jaxpr/rkgd,ckd->kgrc/dot_general | solution.py:27
  109.3 0.0 copy-start.1
  109.3 4.0 %fusion.43 = f32[8,512]{1,0:T(8,128)S(1)} fusion(f32[1024,512,8]{1,0,2:T(8,128)S(1)} %get-tuple-element.334, f32[8,512]{1,0:T(8,128)S(1)} %get-tuple-element.332, pred[512,1024]{0,1:T(8,128)(4,1)S(1)} %compare_and_fusion.2), kind=kLoop, calls=%fused_computation.7.clone.1 | loop fusion | flops 20967424 | bytes 17334272 | tf_op jit(solution)/shard_map/while/body/eval_jaxpr/reduce_sum | solution.py:34
  113.4 0.0 copy-done.1
  113.4 6.1 %bitcast_add_fusion.2 = f32[1,8,512,128]{3,2,1,0:T(8,128)S(1)} fusion(f32[1,8,512,128]{3,2,1,0:T(8,128)S(1)} %copy-done.1, f32[1024,512,8]{1,0,2:T(8,128)S(1)} %get-tuple-element.334, f32[8,512]{1,0:T(8,128)S(1)} %get-tuple-element.332, pred[512,1024]{0,1:T(8,128)(4,1)S(1)} %compare_and_fusion.2, f32[8,512]{1,0:T(8,128)S(1)} %get-tuple-element.336, ...), kind=kOutput, calls=%fused_computation.11.clone.1 | convolution fusion | flops 1096810496 | bytes 21807108 | tf_op jit(solution)/shard_map/while/body/eval_jaxpr/kgrc,ckd->kgrd/dot_general | solution.py:35
  119.6 0.0 copy-start.2
  119.6 1.3 copy-done.2
  120.9 6.2 %gather_fusion = s32[1024]{0:T(1024)S(1)} fusion(s32[2048]{0:T(1024)S(1)} %get-tuple-element.370, s32[1024]{0:T(1024)S(1)} %broadcast_clamp_fusion.2), kind=kCustom, calls=%fused_computation.clone.clone.1 | custom fusion | bytes 12288 | tf_op jit(solution)/shard_map/while/body/eval_jaxpr/jit(_take)/gather | solution.py:95
  127.1 0.8 compare_and_fusion.2
  128.0 2.9 %fusion.41 = (f32[8,512]{1,0:T(8,128)S(1)}, f32[1024,512,8]{1,0,2:T(8,128)S(1)}) fusion(pred[512,1024]{0,1:T(8,128)(4,1)S(1)} %compare_and_fusion.2, bf16[512,1,8,128]{3,0,2,1:T(8,128)(2,1)S(1)} %get-tuple-element.373, bf16[2048,128]{1,0:T(8,128)(2,1)S(1)} %get-tuple-element.372, s32[]{:T(128)S(6)} %select_n.145), kind=kOutput, calls=%fused_computation.5.clone.1 | convolution fusion | flops 1086320640 | bytes 18628612 | tf_op jit(solution)/shard_map/while/body/eval_jaxpr/rkgd,ckd->kgrc/dot_general | solution.py:27
  130.9 0.0 copy-start.1
  130.9 4.0 %fusion.43 = f32[8,512]{1,0:T(8,128)S(1)} fusion(f32[1024,512,8]{1,0,2:T(8,128)S(1)} %get-tuple-element.334, f32[8,512]{1,0:T(8,128)S(1)} %get-tuple-element.332, pred[512,1024]{0,1:T(8,128)(4,1)S(1)} %compare_and_fusion.2), kind=kLoop, calls=%fused_computation.7.clone.1 | loop fusion | flops 20967424 | bytes 17334272 | tf_op jit(solution)/shard_map/while/body/eval_jaxpr/reduce_sum | solution.py:34
  135.0 0.0 copy-done.1
  135.0 6.1 %bitcast_add_fusion.2 = f32[1,8,512,128]{3,2,1,0:T(8,128)S(1)} fusion(f32[1,8,512,128]{3,2,1,0:T(8,128)S(1)} %copy-done.1, f32[1024,512,8]{1,0,2:T(8,128)S(1)} %get-tuple-element.334, f32[8,512]{1,0:T(8,128)S(1)} %get-tuple-element.332, pred[512,1024]{0,1:T(8,128)(4,1)S(1)} %compare_and_fusion.2, f32[8,512]{1,0:T(8,128)S(1)} %get-tuple-element.336, ...), kind=kOutput, calls=%fused_computation.11.clone.1 | convolution fusion | flops 1096810496 | bytes 21807108 | tf_op jit(solution)/shard_map/while/body/eval_jaxpr/kgrc,ckd->kgrd/dot_general | solution.py:35
  141.1 0.0 copy-start.2
  141.2 1.3 copy-done.2
  142.5 2.0 %fusion.26 = bf16[512,1,8,128]{3,0,2,1:T(8,128)(2,1)S(1)} fusion(f32[1,8,512,128]{3,2,1,0:T(8,128)} %get-tuple-element.175, f32[8,512]{1,0:T(8,128)S(1)} %bitcast.122), kind=kLoop, calls=%fused_computation.42 | loop fusion | flops 1048576 | bytes 3162112 | tf_op jit(solution)/shard_map/convert_element_type | solution.py:105
  144.4 0.7 copy.19
  145.1 0.5 convert_element_type.19
  145.6 30.0 %all_to_all.70 = bf16[8,64,1024]{2,1,0:T(8,128)(2,1)S(1)} all-to-all(bf16[8,64,1024]{2,1,0:T(8,128)(2,1)S(1)} %convert_element_type.19), channel_id=1, replica_groups=mesh['head'=8,'kv'=4] {'head'}, dimensions={0} | all-to-all | bytes 2097152 | tf_op jit(solution)/shard_map/all_to_all | solution.py:106
  175.6 1.1 copy.25
  (21 shorter events, 0.2 us)
Async XLA Ops:
  0.0 0.9 copy-start
  1.6 13.1 %all-to-all-start = ((bf16[64,8,128]{2,0,1:T(8,128)(2,1)}), bf16[64,8,128]{2,0,1:T(8,128)(2,1)S(1)}, u32[]{:S(2)}, u32[]{:S(2)}) async-start(bf16[64,8,128]{2,0,1:T(8,128)(2,1)} %copy_bitcast_fusion.2), calls=%async_computation | async-start | bytes 262144 | tf_op jit(solution)/shard_map/all_to_all | solution.py:66
  14.7 10.1 %all-to-all-start.2 = ((bf16[64,8,128]{2,0,1:T(8,128)(2,1)}), bf16[64,8,128]{2,0,1:T(8,128)(2,1)S(1)}, u32[]{:S(2)}, u32[]{:S(2)}) async-start(bf16[64,8,128]{2,0,1:T(8,128)(2,1)} %copy_bitcast_fusion.1), calls=%async_computation.2 | async-start | bytes 262144 | tf_op jit(solution)/shard_map/all_to_all | solution.py:67
  24.8 74.1 %all-to-all-start.1 = ((bf16[64,8,1024]{2,0,1:T(8,128)(2,1)}), bf16[64,8,1024]{2,0,1:T(8,128)(2,1)S(1)}, u32[]{:S(2)}, u32[]{:S(2)}) async-start(bf16[64,8,1024]{2,0,1:T(8,128)(2,1)} %bitcast.93), calls=%async_computation.1 | async-start | bytes 2097152 | tf_op jit(solution)/shard_map/all_to_all | solution.py:65
  109.3 4.1 %copy-start.1 = (f32[1,8,512,128]{3,2,1,0:T(8,128)S(1)}, f32[1,8,512,128]{3,2,1,0:T(8,128)}, u32[]{:S(2)}) copy-start(f32[1,8,512,128]{3,2,1,0:T(8,128)} %get-tuple-element.355) | copy-start | bytes 6291460 | tf_op jit(solution)/shard_map/while
  119.6 1.3 copy-start.2
  130.9 4.1 %copy-start.1 = (f32[1,8,512,128]{3,2,1,0:T(8,128)S(1)}, f32[1,8,512,128]{3,2,1,0:T(8,128)}, u32[]{:S(2)}) copy-start(f32[1,8,512,128]{3,2,1,0:T(8,128)} %get-tuple-element.355) | copy-start | bytes 6291460 | tf_op jit(solution)/shard_map/while
  141.1 1.3 copy-start.2
where the time goes:
time: 177 us
  blocking collectives  94.4 us (53%)
  local copies, waits for them, and re-layouts  28.4 us (16%)
  matrix products  18.1 us (10%)
  starting transfers between devices  13.3 us (8%)
  other arithmetic  11.8 us (7%)
  waiting for transfers between devices  9.58 us (5%)
    unnamed x1, blocking collectives  43.9 us
    all_to_all x1, blocking collectives, local(): lax.all_to_all(result, 'head', split_axis=0, concat_axis=1, tiled=True)  30 us
    gather x2, local copies, waits for them, and re-layouts, one_step(): key_doc = jnp.take(doc_global, key_pos)  12.3 us
    dot_general x2, matrix products, block_terms(): jnp.einsum('kgrc,ckd->kgrd', weights.astype(jnp.bfloat16), value_heads, p...  12.3 us
    all_gather x1, blocking collectives, local(): value_piece = lax.all_gather(value_block, 'kv', axis=0, tiled=True)  11.6 us
    all_gather x1, blocking collectives, local(): key_piece = lax.all_gather(key_block, 'kv', axis=0, tiled=True)  9 us
    reduce_sum x2, other arithmetic, block_terms(): row_total = jnp.sum(weights, axis=-1)  8.05 us
    all_to_all x1, starting transfers between devices, local(): lax.all_to_all(key_send, 'head', split_axis=1, concat_axis=0, tiled=True)  6.35 us
  transfers between devices with their start and end apart: 3, of which 2 were waited for; matrix products, arithmetic and copies ran while one was open for 5% of the time, Pallas kernels for 0%

commit v1 on v0

--- a/solution.py
+++ b/solution.py
@@ -8,6 +8,12 @@
 KEY_VALUE_HEADS = 8
 HEAD_SIZE = 128
 NEG_FILL = -1e30
+
+
+def swap_blocks(block, mesh_axis, split, join):
+    shards = jnp.split(block, lax.axis_size(mesh_axis), axis=split)
+    arrived = lax.all_to_all(jnp.stack(shards), mesh_axis, 0, 0)
+    return jnp.concatenate(arrived, axis=join)
 
 
 def repeat_heads(input_matrix, head_repeats):
@@ -64,7 +70,7 @@
     query_block, key_block, value_block = (
         lax.all_to_all(queries, "head", split_axis=1, concat_axis=0, tiled=True),
         lax.all_to_all(key_send, "head", split_axis=1, concat_axis=0, tiled=True),
-        lax.all_to_all(value_send, "head", split_axis=1, concat_axis=0, tiled=True),
+        swap_blocks(value_send, "head", 1, 0),
     )
     block_len = query_block.shape[0]
     doc_global = lax.all_gather(doc_ids, ("kv", "head"), axis=0, tiled=True)

time: 177 us -> 183 us (1.034)
  local copies, waits for them, and re-layouts: 28.4 us -> 34.6 us
  waiting for transfers between devices: 9.58 us -> 4.47 us
  matrix products: 18.1 us -> 20.2 us
    unnamed x7 -> x14, local copies, waits for them, and re-layouts: 3.49 us -> 12.6 us
    all_to_all x1, waiting for transfers between devices: 5.18 us -> 0.01 us  [local(): lax.all_to_all(key_send, 'head', split_axis=1, concat_axis=0, tiled=True)]
    while x10 -> x2, local copies, waits for them, and re-layouts: 2.68 us -> 0.01 us
    dot_general x2, matrix products: 12.3 us -> 14.4 us  [block_terms(): jnp.einsum('kgrc,ckd->kgrd', weights.astype(jnp.bfloat16), value_heads, p...]
  transfers between devices with their start and end apart: 3 -> 3, of which waited for: 2 -> 1; matrix products, arithmetic and copies ran while one was open for 5% -> 10% of each run, Pallas kernels for 0% -> 0%
where the time goes in v1:
time: 183 us; the launch traced here: 182 us
  blocking collectives  94.6 us (52%)
  local copies, waits for them, and re-layouts  34.6 us (19%)
  matrix products  20.2 us (11%)
  starting transfers between devices  15 us (8%)
  other arithmetic  11.8 us (6%)
  waiting for transfers between devices  4.47 us (2%)
    unnamed x1, blocking collectives  44.1 us
    all_to_all x1, blocking collectives, local(): lax.all_to_all(result, 'head', split_axis=0, concat_axis=1, tiled=True)  30 us
    dot_general x2, matrix products, block_terms(): jnp.einsum('kgrc,ckd->kgrd', weights.astype(jnp.bfloat16), value_heads, p...  14.4 us
    unnamed x14, local copies, waits for them, and re-layouts  12.6 us
    gather x2, local copies, waits for them, and re-layouts, one_step(): key_doc = jnp.take(doc_global, key_pos)  12.3 us
    all_gather x1, blocking collectives, local(): value_piece = lax.all_gather(value_block, 'kv', axis=0, tiled=True)  11.6 us
    all_gather x1, blocking collectives, local(): key_piece = lax.all_gather(key_block, 'kv', axis=0, tiled=True)  9 us
    reduce_sum x2, other arithmetic, block_terms(): row_total = jnp.sum(weights, axis=-1)  8.05 us
  transfers between devices with their start and end apart: 3, of which 1 were waited for; matrix products, arithmetic and copies ran while one was open for 10% of the time, Pallas kernels for 0%

profile of v1, /device:TPU:0, one launch (start us, length us, event | category | flops | bytes accessed | tf_op | source)
XLA Modules:
  0.0 181.6 jit_solution(3909484319638333116)
XLA Ops:
  0.0 0.0 copy-start
  0.0 0.9 copy-done
  0.9 0.7 copy_bitcast_fusion.1
  1.6 6.4 %all-to-all-start = ((bf16[64,8,128]{2,0,1:T(8,128)(2,1)}), bf16[64,8,128]{2,0,1:T(8,128)(2,1)S(1)}, u32[]{:S(2)}, u32[]{:S(2)}) async-start(bf16[64,8,128]{2,0,1:T(8,128)(2,1)} %copy_bitcast_fusion.1), calls=%async_computation | async-start | bytes 262144 | tf_op jit(solution)/shard_map/all_to_all | solution.py:72
  7.9 1.3 constant_dynamic-update-slice_fusion.7
  9.3 1.3 constant_dynamic-update-slice_fusion.6
  10.6 1.3 constant_dynamic-update-slice_fusion.5
  11.9 1.3 constant_dynamic-update-slice_fusion.4
  13.2 1.3 constant_dynamic-update-slice_fusion.3
  14.5 1.3 constant_dynamic-update-slice_fusion.2
  15.8 1.3 constant_dynamic-update-slice_fusion.1
  17.2 1.3 constant_dynamic-update-slice_fusion
  18.5 0.0 all-to-all-done
  18.5 5.1 %all-to-all-start.2 = ((bf16[8,64,128]{2,1,0:T(8,128)(2,1)}), bf16[8,64,128]{2,1,0:T(8,128)(2,1)S(1)}, u32[]{:S(2)}, u32[]{:S(2)}) async-start(bf16[8,64,128]{2,1,0:T(8,128)(2,1)} %constant_dynamic-update-slice_fusion), calls=%async_computation.2 | async-start | bytes 262144 | tf_op jit(solution)/shard_map/all_to_all | solution.py:15
  23.6 2.3 %copy.25 = bf16[8,8,8,1024]{3,2,0,1:T(8,128)(2,1)} copy(bf16[8,8,8,1024]{3,2,1,0:T(8,128)(2,1)} %bitcast.130) | data formatting | bytes 2097152 | tf_op jit(solution)/shard_map/all_to_all | solution.py:71
  25.9 4.5 %all-to-all-done.2 = bf16[8,64,128]{2,1,0:T(8,128)(2,1)S(1)} async-done(((bf16[8,64,128]{2,1,0:T(8,128)(2,1)}), bf16[8,64,128]{2,1,0:T(8,128)(2,1)S(1)}, u32[]{:S(2)}, u32[]{:S(2)}) %all-to-all-start.2) | async-done | bytes 131104 | tf_op jit(solution)/shard_map/all_to_all | solution.py:15
  30.3 3.6 %all-to-all-start.1 = ((bf16[64,8,1024]{2,0,1:T(8,128)(2,1)}), bf16[64,8,1024]{2,0,1:T(8,128)(2,1)S(1)}, u32[]{:S(2)}, u32[]{:S(2)}) async-start(bf16[64,8,1024]{2,0,1:T(8,128)(2,1)} %bitcast.102), calls=%async_computation.1 | async-start | bytes 2097152 | tf_op jit(solution)/shard_map/all_to_all | solution.py:71
  33.9 1.2 dynamic-slice
  35.8 0.9 dynamic-update-slice
  36.6 44.1 %all-reduce = s32[2048]{0:T(1024)S(1)} all-reduce(s32[2048]{0:T(1024)S(1)} %dynamic-update-slice), channel_id=1, replica_groups=mesh['head'=8,'kv'=4] {'kv','head'}, use_global_device_ids=true, to_apply=%add | all-reduce | flops 2048 | bytes 16384
  80.7 3.1 %gather_fusion.1 = s32[512]{0:T(512)S(1)} fusion(s32[2048]{0:T(1024)S(1)} %all-reduce, s32[1024]{0:T(1024)S(1)} %pad_clamp_fusion), kind=kCustom, calls=%fused_computation.1 | custom fusion | bytes 6144 | tf_op jit(solution)/shard_map/jit(_take)/gather | solution.py:83
  83.9 11.6 %all_gather.11 = bf16[2048,128]{1,0:T(8,128)(2,1)S(1)} all-gather(bf16[512,128]{1,0:T(8,128)(2,1)S(1)} %bitcast.133), channel_id=1, replica_groups=mesh['head'=8,'kv'=4] {'kv'}, dimensions={0}, use_global_device_ids=true | all-gather | bytes 655360 | tf_op jit(solution)/shard_map/all_gather | solution.py:92
  95.5 9.0 %all_gather.10 = bf16[2048,128]{1,0:T(8,128)(2,1)S(1)} all-gather(bf16[512,128]{1,0:T(8,128)(2,1)S(1)} %bitcast.132), channel_id=1, replica_groups=mesh['head'=8,'kv'=4] {'kv'}, dimensions={0}, use_global_device_ids=true | all-gather | bytes 655360 | tf_op jit(solution)/shard_map/all_gather | solution.py:91
  104.5 0.0 all-to-all-done.1
  104.5 0.3 copy.22
  104.8 0.1 copy.15
  104.9 42.6 %while.18 = (s32[]{:T(128)}, f32[1,8,512]{2,1,0:T(8,128)S(1)}, f32[1,8,512]{2,1,0:T(8,128)S(1)}, f32[1,8,512,128]{3,2,1,0:T(8,128)}, s32[2048]{0:T(1024)S(1)}, /...) while((s32[]{:T(128)}, f32[1,8,512]{2,1,0:T(8,128)S(1)}, ...), condition=%wide.region_3.4_spmd.clone, body=%wide.region_0.3_spmd.clone.sunk | while | flops 2205726208 | bytes 58558680 | solution.py:107
  105.0 6.2 %gather_fusion = s32[1024]{0:T(1024)S(1)} fusion(s32[2048]{0:T(1024)S(1)} %get-tuple-element.370, s32[1024]{0:T(1024)S(1)} %broadcast_clamp_fusion.2), kind=kCustom, calls=%fused_computation.clone.clone.1 | custom fusion | bytes 12288 | tf_op jit(solution)/shard_map/while/body/eval_jaxpr/jit(_take)/gather | solution.py:101
  111.1 0.8 compare_and_fusion.2
  112.0 2.9 %fusion.40 = (f32[8,512]{1,0:T(8,128)S(1)}, f32[1024,512,8]{1,0,2:T(8,128)S(1)}) fusion(pred[512,1024]{0,1:T(8,128)(4,1)S(1)} %compare_and_fusion.2, bf16[512,1,8,128]{3,0,2,1:T(8,128)(2,1)S(1)} %get-tuple-element.373, bf16[2048,128]{1,0:T(8,128)(2,1)S(1)} %get-tuple-element.372, s32[]{:T(128)S(6)} %select_n.145), kind=kOutput, calls=%fused_computation.5.clone.1 | convolution fusion | flops 1086320640 | bytes 18628612 | tf_op jit(solution)/shard_map/while/body/eval_jaxpr/rkgd,ckd->kgrc/dot_general | solution.py:33
  114.9 4.0 %fusion.42 = f32[8,512]{1,0:T(8,128)S(1)} fusion(f32[1024,512,8]{1,0,2:T(8,128)S(1)} %get-tuple-element.334, f32[8,512]{1,0:T(8,128)S(1)} %get-tuple-element.332, pred[512,1024]{0,1:T(8,128)(4,1)S(1)} %compare_and_fusion.2), kind=kLoop, calls=%fused_computation.7.clone.1 | loop fusion | flops 20967424 | bytes 17334272 | tf_op jit(solution)/shard_map/while/body/eval_jaxpr/reduce_sum | solution.py:40
  119.0 6.7 %bitcast_add_fusion.2 = f32[1,8,512,128]{3,2,1,0:T(8,128)} fusion(f32[1,8,512,128]{3,2,1,0:T(8,128)} %get-tuple-element.355, f32[1024,512,8]{1,0,2:T(8,128)S(1)} %get-tuple-element.334, f32[8,512]{1,0:T(8,128)S(1)} %get-tuple-element.332, pred[512,1024]{0,1:T(8,128)(4,1)S(1)} %compare_and_fusion.2, f32[8,512]{1,0:T(8,128)S(1)} %get-tuple-element.336, ...), kind=kOutput, calls=%fused_computation.11.clone.1 | convolution fusion | flops 1096810496 | bytes 21807108 | tf_op jit(solution)/shard_map/while/body/eval_jaxpr/kgrc,ckd->kgrd/dot_general | solution.py:41
  125.7 6.2 %gather_fusion = s32[1024]{0:T(1024)S(1)} fusion(s32[2048]{0:T(1024)S(1)} %get-tuple-element.370, s32[1024]{0:T(1024)S(1)} %broadcast_clamp_fusion.2), kind=kCustom, calls=%fused_computation.clone.clone.1 | custom fusion | bytes 12288 | tf_op jit(solution)/shard_map/while/body/eval_jaxpr/jit(_take)/gather | solution.py:101
  131.9 0.8 compare_and_fusion.2
  132.8 2.9 %fusion.40 = (f32[8,512]{1,0:T(8,128)S(1)}, f32[1024,512,8]{1,0,2:T(8,128)S(1)}) fusion(pred[512,1024]{0,1:T(8,128)(4,1)S(1)} %compare_and_fusion.2, bf16[512,1,8,128]{3,0,2,1:T(8,128)(2,1)S(1)} %get-tuple-element.373, bf16[2048,128]{1,0:T(8,128)(2,1)S(1)} %get-tuple-element.372, s32[]{:T(128)S(6)} %select_n.145), kind=kOutput, calls=%fused_computation.5.clone.1 | convolution fusion | flops 1086320640 | bytes 18628612 | tf_op jit(solution)/shard_map/while/body/eval_jaxpr/rkgd,ckd->kgrc/dot_general | solution.py:33
  135.7 4.0 %fusion.42 = f32[8,512]{1,0:T(8,128)S(1)} fusion(f32[1024,512,8]{1,0,2:T(8,128)S(1)} %get-tuple-element.334, f32[8,512]{1,0:T(8,128)S(1)} %get-tuple-element.332, pred[512,1024]{0,1:T(8,128)(4,1)S(1)} %compare_and_fusion.2), kind=kLoop, calls=%fused_computation.7.clone.1 | loop fusion | flops 20967424 | bytes 17334272 | tf_op jit(solution)/shard_map/while/body/eval_jaxpr/reduce_sum | solution.py:40
  139.8 7.7 %bitcast_add_fusion.2 = f32[1,8,512,128]{3,2,1,0:T(8,128)} fusion(f32[1,8,512,128]{3,2,1,0:T(8,128)} %get-tuple-element.355, f32[1024,512,8]{1,0,2:T(8,128)S(1)} %get-tuple-element.334, f32[8,512]{1,0:T(8,128)S(1)} %get-tuple-element.332, pred[512,1024]{0,1:T(8,128)(4,1)S(1)} %compare_and_fusion.2, f32[8,512]{1,0:T(8,128)S(1)} %get-tuple-element.336, ...), kind=kOutput, calls=%fused_computation.11.clone.1 | convolution fusion | flops 1096810496 | bytes 21807108 | tf_op jit(solution)/shard_map/while/body/eval_jaxpr/kgrc,ckd->kgrd/dot_general | solution.py:41
  147.5 2.0 %fusion.26 = bf16[512,1,8,128]{3,0,2,1:T(8,128)(2,1)S(1)} fusion(f32[1,8,512,128]{3,2,1,0:T(8,128)} %get-tuple-element.175, f32[8,512]{1,0:T(8,128)S(1)} %bitcast.131), kind=kLoop, calls=%fused_computation.42 | loop fusion | flops 1048576 | bytes 3162112 | tf_op jit(solution)/shard_map/convert_element_type | solution.py:111
  149.4 0.7 copy.16
  150.1 0.5 convert_element_type.19
  150.6 30.0 %all_to_all.56 = bf16[8,64,1024]{2,1,0:T(8,128)(2,1)S(1)} all-to-all(bf16[8,64,1024]{2,1,0:T(8,128)(2,1)S(1)} %convert_element_type.19), channel_id=1, replica_groups=mesh['head'=8,'kv'=4] {'head'}, dimensions={0} | all-to-all | bytes 2097152 | tf_op jit(solution)/shard_map/all_to_all | solution.py:112
  180.6 1.1 copy.21
  (21 shorter events, 0.2 us)
Async XLA Ops:
  0.0 0.9 copy-start
  1.6 16.9 %all-to-all-start = ((bf16[64,8,128]{2,0,1:T(8,128)(2,1)}), bf16[64,8,128]{2,0,1:T(8,128)(2,1)S(1)}, u32[]{:S(2)}, u32[]{:S(2)}) async-start(bf16[64,8,128]{2,0,1:T(8,128)(2,1)} %copy_bitcast_fusion.1), calls=%async_computation | async-start | bytes 262144 | tf_op jit(solution)/shard_map/all_to_all | solution.py:72
  18.5 11.8 %all-to-all-start.2 = ((bf16[8,64,128]{2,1,0:T(8,128)(2,1)}), bf16[8,64,128]{2,1,0:T(8,128)(2,1)S(1)}, u32[]{:S(2)}, u32[]{:S(2)}) async-start(bf16[8,64,128]{2,1,0:T(8,128)(2,1)} %constant_dynamic-update-slice_fusion), calls=%async_computation.2 | async-start | bytes 262144 | tf_op jit(solution)/shard_map/all_to_all | solution.py:15
  30.3 74.1 %all-to-all-start.1 = ((bf16[64,8,1024]{2,0,1:T(8,128)(2,1)}), bf16[64,8,1024]{2,0,1:T(8,128)(2,1)S(1)}, u32[]{:S(2)}, u32[]{:S(2)}) async-start(bf16[64,8,1024]{2,0,1:T(8,128)(2,1)} %bitcast.102), calls=%async_computation.1 | async-start | bytes 2097152 | tf_op jit(solution)/shard_map/all_to_all | solution.py:71
